TPU v7x, 256 devices: a whole 4x4x8 slice. The times are simulated.
256 devices in a mesh: band: 16 (over y_lo, x, core), grid: 16 (over y_hi, z).
Axes of the slice: x: 4, y: 4 (y_hi: 2, y_lo: 2; y = y_hi * 2 + y_lo), z: 8, core: 2. Of those that a mesh axis runs over, the one named last changes fastest.
Arguments:
- orbitals: float32 [64, 48, 2304], P('band', 'grid'), may hold values from -5.5 to 6.6
- occupation: int32 [64], P('band'), may hold values from 0 to 2
- cutoff: int32 [], replicated, may hold values from 144 to 1728
Outputs:
- exchange_term: float32 [64, 48, 2304], P('band', 'grid')
All inputs are finite; a program needn't handle non-finite values.
Results may differ from a plain program's by a relative error of at most 0.00005.
Values sent between devices are 32-bit elements; how exact they have to be, the bound alone decides.
No kernel may reach another device: no remote copies, remote signals or barrier semaphores. Data moves between devices by JAX's collectives and lax.ppermute only.
A program may use at most 128 MiB of HBM per device.

v0:
```python
import jax
import jax.numpy as jnp
from jax import lax
from jax.sharding import PartitionSpec as P

G = 48
screen_alpha = 2.0
screen_scale = 4.0


def shifted(block, axis, distance):
    devices = range(lax.axis_size(axis))
    route = [((i - distance) % len(devices), i) for i in devices]
    return lax.ppermute(block, axis, route)


def transform_tables(extent, cutoff):
    position = jnp.arange(extent, dtype=jnp.int32)
    middle = extent // 2
    frequency = jnp.where(position <= middle, position, position - middle)
    phase_index = frequency[:, None] * position[None, :] % extent
    angles = 2.0 * jnp.pi / extent * phase_index.astype(jnp.float32)
    transform = jnp.where((position <= middle)[:, None], jnp.cos(angles), jnp.sin(angles))
    weight = jnp.where((position == 0) | (position == middle), 1.0, 2.0).astype(jnp.float32)
    shells = (
        frequency[:, None, None] ** 2
        + frequency[None, :, None] ** 2
        + frequency[None, None, :] ** 2
    )
    ratios = shells.astype(jnp.float32) / screen_alpha
    screen = jnp.where(
        shells > 0, (1.0 - jnp.exp(-ratios)) / jnp.maximum(ratios, 1.0 / screen_alpha), 1.0
    )
    factor = weight[:, None, None] * weight[None, :, None] * weight[None, None, :]
    kernel = jnp.where(shells <= cutoff, screen_scale * screen * factor / float(extent**3), 0.0)
    return (transform, kernel.reshape(extent, extent * extent))


def apply_transform(matrix, fields):
    batch_size, extent, row_cells = fields.shape
    first = jnp.matmul(matrix, fields, precision=lax.Precision.HIGHEST)
    second = jnp.matmul(
        matrix, first.reshape(batch_size * extent, extent, extent), precision=lax.Precision.HIGHEST
    )
    third = jnp.matmul(
        second.reshape(batch_size * extent * extent, extent),
        matrix.T,
        precision=lax.Precision.HIGHEST,
    )
    return third.reshape(batch_size, extent, row_cells)


def screened_potential(fields, transform, kernel):
    spectrum = apply_transform(transform, fields) * kernel[None]
    return apply_transform(transform.T, spectrum)


def solve_pairs(densities, transform, kernel):
    groups = lax.axis_size("grid")
    pair_count, planes, row_cells = densities.shape
    shaped = densities.reshape(groups, pair_count // groups, planes, row_cells)
    pieces = lax.all_to_all(shaped, "grid", split_axis=0, concat_axis=2, tiled=True)
    fields = pieces.reshape(pieces.shape[1], pieces.shape[2], pieces.shape[3])
    potential = screened_potential(fields, transform, kernel).reshape(pieces.shape)
    sliced = lax.all_to_all(potential, "grid", split_axis=2, concat_axis=0, tiled=True)
    return sliced.reshape(pair_count, planes, row_cells)


def pair_densities(home_orbitals, visitor_orbitals):
    orbital_count, planes, row_cells = home_orbitals.shape
    products = home_orbitals[:, None] * visitor_orbitals[None, :]
    return products.reshape(orbital_count * orbital_count, planes, row_cells)


def pair_terms(home_orbitals, home_weights, visitor_orbitals, visitor_weights, potentials):
    orbital_count, planes, row_cells = home_orbitals.shape
    shaped = potentials.reshape(orbital_count, orbital_count, planes, row_cells)
    scaled_visitor = visitor_weights[:, None, None] * visitor_orbitals
    scaled_home = home_weights[:, None, None] * home_orbitals
    to_home = jnp.sum(scaled_visitor[None] * shaped, axis=1)
    to_visitor = jnp.sum(scaled_home[:, None] * shaped, axis=0)
    return (to_home, to_visitor)


def on_device(orbitals, occupation, cutoff):
    transform, kernel = transform_tables(G, cutoff)
    weights = occupation.astype(jnp.float32) * 0.5
    half_cycle = lax.axis_size("band") // 2
    blocks = [(orbitals, weights)]
    visitor = (orbitals, weights)
    for distance in range(1, half_cycle + 1):
        visitor = shifted((orbitals, weights), "band", distance)
        blocks.append(visitor)
    densities = jnp.concatenate([pair_densities(orbitals, member[0]) for member in blocks], axis=0)
    potentials = solve_pairs(densities, transform, kernel)
    per_set = potentials.reshape(half_cycle + 1, -1, potentials.shape[1], potentials.shape[2])
    applied = jnp.zeros_like(orbitals)
    for distance in range(half_cycle + 1):
        member = blocks[distance]
        to_home, to_visitor = pair_terms(orbitals, weights, member[0], member[1], per_set[distance])
        applied = applied + to_home
        if 0 < distance < half_cycle:
            applied = applied + shifted(to_visitor, "band", -distance)
    return -applied


def solution(mesh):
    placed = (P("band", "grid", None), P("band"), P())
    return jax.shard_map(
        on_device, mesh=mesh, in_specs=placed, out_specs=P("band", "grid", None), check_vma=False
    )
```

profile of v0, /device:TPU:7, one launch (start us, length us, event | category | flops | bytes accessed | tf_op | source)
XLA Modules:
  0.0 483.2 jit_solution(18098811238183727219)
XLA Ops:
  0.0 1.8 collective-permute-start
  1.8 1.2 collective-permute-start.1
  3.0 1.2 collective-permute-start.2
  4.2 2.4 collective-permute-start.3
  6.6 1.7 collective-permute-start.5
  8.3 1.2 collective-permute-start.6
  9.6 0.5 collective-permute-start.7
  10.1 1.0 copy.121
  11.3 2.4 collective-permute-done.4
  13.7 2.9 collective-permute-done.5
  16.7 0.4 collective-permute-done.6
  17.2 1.2 broadcast_multiply_fusion
  18.5 0.1 constant_dynamic-update-slice_fusion.7
  18.6 0.1 constant_dynamic-update-slice_fusion.6
  19.7 2.3 copy-done
  22.0 10.4 %all-to-all-start = ((f32[16,9,3,2304]{3,2,1,0:T(4,128)}), f32[16,9,3,2304]{3,2,1,0:T(4,128)}, u32[]{:S(2)}, u32[]{:S(2)}) async-start(f32[16,9,3,2304]{3,2,1,0:T(4,128)} %bitcast.56), calls=%async_computation | async-start | bytes 10616832 | tf_op jit(solution)/shard_map/all_to_all | solution.py:62
  32.5 0.4 add.137
  32.9 0.5 add.138
  33.5 0.4 mul.585
  33.9 0.5 mul.586
  35.2 0.3 multiply_select_fusion
  35.5 118.0 %all-to-all-done = f32[16,9,3,2304]{3,2,1,0:T(4,128)} async-done(((f32[16,9,3,2304]{3,2,1,0:T(4,128)}), f32[16,9,3,2304]{3,2,1,0:T(4,128)}, u32[]{:S(2)}, u32[]{:S(2)}) %all-to-all-start) | async-done | bytes 3981344 | tf_op jit(solution)/shard_map/all_to_all | solution.py:62
  153.5 5.9 %copy.131 = f32[1,9,16,3,2304]{4,3,2,1,0:T(4,128)} copy(f32[1,9,16,3,2304]{4,3,1,2,0:T(4,128)} %bitcast.14) | data formatting | bytes 7962624 | tf_op jit(solution)/shard_map/all_to_all | solution.py:62
  159.4 6.7 %reshape.334 = f32[9,48,2304]{2,1,0:T(8,128)} reshape(f32[1,9,16,3,2304]{4,3,2,1,0:T(4,128)} %copy.131) | data formatting | bytes 7962624 | tf_op jit(solution)/shard_map/reshape | solution.py:63
  166.2 7.7 %convolution_bitcast_fusion.1 = f32[9,48,2304]{2,1,0:T(8,128)} fusion(f32[9,48,2304]{2,1,0:T(8,128)} %reshape.334, s32[48]{0:T(128)S(1)} %add_select_fusion.1, pred[48]{0:T(512)(128)(4,1)S(1)} %iota_compare_fusion), kind=kOutput, calls=%fused_computation.1 | convolution fusion | flops 573331968 | bytes 7962864 | tf_op jit(solution)/shard_map/dot_general | solution.py:41
  173.9 10.3 %reshape.335 = f32[432,48,48]{2,1,0:T(8,128)} reshape(f32[9,48,2304]{2,1,0:T(8,128)} %convolution_bitcast_fusion.1) | data formatting | bytes 7962624 | tf_op jit(solution)/shard_map/reshape | solution.py:43
  184.2 9.5 %copy.134 = f32[432,48,48]{0,1,2:T(8,128)} copy(f32[432,48,48]{2,1,0:T(8,128)} %reshape.335) | data formatting | bytes 7962624 | tf_op jit(solution)/shard_map/reshape | solution.py:43
  193.6 7.6 %convolution_bitcast_fusion.3 = f32[432,48,48]{0,1,2:T(8,128)} fusion(f32[432,48,48]{0,1,2:T(8,128)} %copy.134, s32[48]{0:T(128)S(1)} %add_select_fusion.1, pred[48]{0:T(512)(128)(4,1)S(1)} %iota_compare_fusion), kind=kOutput, calls=%fused_computation.4 | convolution fusion | flops 573331968 | bytes 7962864 | tf_op jit(solution)/shard_map/dot_general | solution.py:42
  201.3 8.5 %copy.135 = f32[432,48,48]{1,0,2:T(8,128)} copy(f32[432,48,48]{0,1,2:T(8,128)} %convolution_bitcast_fusion.3) | data formatting | bytes 7962624 | tf_op jit(solution)/shard_map/transpose | solution.py:42
  209.7 9.3 %reshape.336 = f32[20736,48]{0,1:T(8,128)} reshape(f32[432,48,48]{1,0,2:T(8,128)} %copy.135) | data formatting | bytes 7962624 | tf_op jit(solution)/shard_map/reshape | solution.py:46
  219.0 20.2 %fusion.11 = f32[20736,48]{1,0:T(8,128)} fusion(f32[20736,48]{0,1:T(8,128)} %reshape.336, s32[48]{0:T(128)S(1)} %add_select_fusion.1, pred[48]{0:T(512)(128)(4,1)S(1)} %iota_compare_fusion), kind=kOutput, calls=%fused_computation.65 | convolution fusion | flops 573331968 | bytes 7962864 | tf_op jit(solution)/shard_map/dot_general | solution.py:45
  239.2 9.5 %reshape.337 = f32[9,48,2304]{2,1,0:T(8,128)} reshape(f32[20736,48]{1,0:T(8,128)} %fusion.11) | data formatting | bytes 7962624 | tf_op jit(solution)/shard_map/reshape | solution.py:50
  248.7 7.7 %convolution_bitcast_fusion = f32[9,48,2304]{2,1,0:T(8,128)} fusion(f32[9,48,2304]{2,1,0:T(8,128)} %reshape.337, f32[48,2304]{1,0:T(8,128)S(1)} %multiply_select_fusion, s32[48]{0:T(128)S(1)} %add_select_fusion.1, pred[48]{0:T(512)(128)(4,1)S(1)} %iota_compare_fusion), kind=kOutput, calls=%fused_computation | convolution fusion | flops 574327296 | bytes 8405232 | tf_op jit(solution)/shard_map/dot_general | solution.py:41
  256.4 10.7 %reshape.338 = f32[432,48,48]{2,1,0:T(8,128)} reshape(f32[9,48,2304]{2,1,0:T(8,128)} %convolution_bitcast_fusion) | data formatting | bytes 7962624 | tf_op jit(solution)/shard_map/reshape | solution.py:43
  267.1 9.5 %copy.137 = f32[432,48,48]{0,1,2:T(8,128)} copy(f32[432,48,48]{2,1,0:T(8,128)} %reshape.338) | data formatting | bytes 7962624 | tf_op jit(solution)/shard_map/reshape | solution.py:43
  276.5 8.6 %convolution_bitcast_fusion.2 = f32[432,48,48]{0,1,2:T(8,128)} fusion(f32[432,48,48]{0,1,2:T(8,128)} %copy.137, s32[48]{0:T(128)S(1)} %add_select_fusion.1, pred[48]{0:T(512)(128)(4,1)S(1)} %iota_compare_fusion), kind=kOutput, calls=%fused_computation.3 | convolution fusion | flops 573331968 | bytes 7962864 | tf_op jit(solution)/shard_map/dot_general | solution.py:42
  285.2 8.5 %copy.138 = f32[432,48,48]{1,0,2:T(8,128)} copy(f32[432,48,48]{0,1,2:T(8,128)} %convolution_bitcast_fusion.2) | data formatting | bytes 7962624 | tf_op jit(solution)/shard_map/transpose | solution.py:42
  293.6 9.1 %reshape.339 = f32[20736,48]{0,1:T(8,128)} reshape(f32[432,48,48]{1,0,2:T(8,128)} %copy.138) | data formatting | bytes 7962624 | tf_op jit(solution)/shard_map/reshape | solution.py:46
  302.7 20.3 %fusion.12 = f32[20736,48]{1,0:T(8,128)} fusion(f32[20736,48]{0,1:T(8,128)} %reshape.339, s32[48]{0:T(128)S(1)} %add_select_fusion.1, pred[48]{0:T(512)(128)(4,1)S(1)} %iota_compare_fusion), kind=kOutput, calls=%fused_computation.66 | convolution fusion | flops 573331968 | bytes 7962864 | tf_op jit(solution)/shard_map/dot_general | solution.py:45
  323.1 9.5 %reshape_reshape.6 = f32[1,9,48,2304]{3,2,1,0:T(8,128)} reshape(f32[20736,48]{1,0:T(8,128)} %fusion.12) | data formatting | bytes 7962624 | tf_op jit(solution)/shard_map/reshape;reshape | solution.py:64
  332.6 8.1 %copy.140 = f32[1,9,48,2304]{3,0,1,2:T(1,128)} copy(f32[1,9,48,2304]{3,2,1,0:T(8,128)} %reshape_reshape.6) | data formatting | bytes 7962624 | tf_op jit(solution)/shard_map/reshape;reshape | solution.py:64
  340.7 10.1 %all-to-all-start.1 = ((f32[1,9,48,2304]{3,0,1,2:T(1,128)}), f32[1,9,48,2304]{3,0,1,2:T(1,128)}, u32[]{:S(2)}, u32[]{:S(2)}) async-start(f32[1,9,48,2304]{3,0,1,2:T(1,128)} %copy.140), calls=%async_computation.1 | async-start | bytes 7962624 | tf_op jit(solution)/shard_map/all_to_all | solution.py:65
  350.8 7.1 %collective-permute-start.8 = (f32[4]{0:T(128)S(1)}, f32[4]{0:T(128)S(1)}, u32[]{:S(2)}, u32[]{:S(2)}) collective-permute-start(f32[4]{0:T(128)S(1)} %convert_multiply_fusion), channel_id=1, source_target_pairs={{240,0},{0,16},{16,32},{32,48},{48,64},{64,80},{80,96},{96,112},{1... | collective-permute-start | bytes 56 | tf_op jit(solution)/shard_map/ppermute | solution.py:14
  357.9 4.4 collective-permute-start.14
  362.7 2.9 collective-permute-start.20
  365.8 0.2 collective-permute-start.22
  366.2 1.0 collective-permute-done.16
  367.5 0.4 collective-permute-done.20
  368.0 74.5 %all-to-all-done.1 = f32[1,9,48,2304]{3,0,1,2:T(1,128)} async-done(((f32[1,9,48,2304]{3,0,1,2:T(1,128)}), f32[1,9,48,2304]{3,0,1,2:T(1,128)}, u32[]{:S(2)}, u32[]{:S(2)}) %all-to-all-start.1) | async-done | bytes 3981344 | tf_op jit(solution)/shard_map/all_to_all | solution.py:65
  442.5 5.3 %copy.141 = f32[1,9,48,2304]{3,0,2,1:T(1,128)S(1)} copy(f32[1,9,48,2304]{3,0,1,2:T(1,128)} %all-to-all-done.1) | data formatting | bytes 7962624 | tf_op jit(solution)/shard_map/all_to_all | solution.py:65
  447.8 1.4 copy.142
  449.2 1.1 fusion.32
  450.3 2.9 multiply_reduce_fusion.14
  453.3 4.9 %collective-permute-start.13 = (f32[4,3,2304]{2,1,0:T(4,128)S(1)}, f32[4,3,2304]{2,1,0:T(4,128)S(1)}, u32[]{:S(2)}, u32[]{:S(2)}) collective-permute-start(f32[4,3,2304]{2,1,0:T(4,128)S(1)} %get-tuple-element.29), channel_id=1, source_target_pairs={{48,0},{64,16},{80,32},{96,48},{112,64},{128,80},{144,96},{160,112... | collective-permute-start | bytes 331784 | tf_op jit(solution)/shard_map/ppermute | solution.py:14
  458.3 4.0 collective-permute-start.15
  462.3 0.5 collective-permute-start.17
  462.8 1.7 collective-permute-start.19
  464.5 3.0 collective-permute-start.21
  467.5 4.1 collective-permute-done.13
  471.6 0.1 multiply_reduce_fusion
  471.8 5.5 %collective-permute-done.19 = f32[4,3,2304]{2,1,0:T(4,128)S(1)} collective-permute-done((f32[4,3,2304]{2,1,0:T(4,128)S(1)}, f32[4,3,2304]{2,1,0:T(4,128)S(1)}, u32[]{:S(2)}, u32[]{:S(2)}) %collective-permute-start.19) | collective-permute-done | bytes 110624 | tf_op jit(solution)/shard_map/ppermute | solution.py:14
  477.3 4.5 collective-permute-done.21
  481.8 0.3 add_negate_fusion
  482.1 0.7 copy.152
  (71 shorter events, 2.9 us)
Async XLA Ops:
  0.0 6.6 %collective-permute-start = (f32[4,3,2304]{2,0,1:T(4,128)}, f32[4,3,2304]{2,0,1:T(4,128)S(1)}, u32[]{:S(2)}, u32[]{:S(2)}) collective-permute-start(f32[4,3,2304]{2,0,1:T(4,128)} %param.3), channel_id=1, source_target_pairs={{240,0},{0,16},{16,32},{32,48},{48,64},{64,80},{80,96},{96,112},{1... | collective-permute-start | bytes 331784 | tf_op jit(solution)/shard_map/ppermute | solution.py:14
  1.8 6.5 %collective-permute-start.1 = (f32[4,3,2304]{2,0,1:T(4,128)}, f32[4,3,2304]{2,0,1:T(4,128)S(1)}, u32[]{:S(2)}, u32[]{:S(2)}) collective-permute-start(f32[4,3,2304]{2,0,1:T(4,128)} %param.3), channel_id=1, source_target_pairs={{224,0},{240,16},{0,32},{16,48},{32,64},{48,80},{64,96},{80,112},{... | collective-permute-start | bytes 331784 | tf_op jit(solution)/shard_map/ppermute | solution.py:14
  3.0 6.6 %collective-permute-start.2 = (f32[4,3,2304]{2,0,1:T(4,128)}, f32[4,3,2304]{2,0,1:T(4,128)S(1)}, u32[]{:S(2)}, u32[]{:S(2)}) collective-permute-start(f32[4,3,2304]{2,0,1:T(4,128)} %param.3), channel_id=1, source_target_pairs={{208,0},{224,16},{240,32},{0,48},{16,64},{32,80},{48,96},{64,112},... | collective-permute-start | bytes 331784 | tf_op jit(solution)/shard_map/ppermute | solution.py:14
  4.2 7.0 %collective-permute-start.3 = (f32[4,3,2304]{2,0,1:T(4,128)}, f32[4,3,2304]{2,0,1:T(4,128)S(1)}, u32[]{:S(2)}, u32[]{:S(2)}) collective-permute-start(f32[4,3,2304]{2,0,1:T(4,128)} %param.3), channel_id=1, source_target_pairs={{192,0},{208,16},{224,32},{240,48},{0,64},{16,80},{32,96},{48,112}... | collective-permute-start | bytes 331784 | tf_op jit(solution)/shard_map/ppermute | solution.py:14
  6.6 7.1 %collective-permute-start.4 = (f32[4,3,2304]{2,0,1:T(4,128)}, f32[4,3,2304]{2,0,1:T(4,128)S(1)}, u32[]{:S(2)}, u32[]{:S(2)}) collective-permute-start(f32[4,3,2304]{2,0,1:T(4,128)} %param.3), channel_id=1, source_target_pairs={{176,0},{192,16},{208,32},{224,48},{240,64},{0,80},{16,96},{32,112... | collective-permute-start | bytes 331784 | tf_op jit(solution)/shard_map/ppermute | solution.py:14
  6.6 10.0 %collective-permute-start.5 = (f32[4,3,2304]{2,0,1:T(4,128)}, f32[4,3,2304]{2,0,1:T(4,128)S(1)}, u32[]{:S(2)}, u32[]{:S(2)}) collective-permute-start(f32[4,3,2304]{2,0,1:T(4,128)} %param.3), channel_id=1, source_target_pairs={{160,0},{176,16},{192,32},{208,48},{224,64},{240,80},{0,96},{16,11... | collective-permute-start | bytes 331784 | tf_op jit(solution)/shard_map/ppermute | solution.py:14
  8.3 8.8 %collective-permute-start.6 = (f32[4,3,2304]{2,0,1:T(4,128)}, f32[4,3,2304]{2,0,1:T(4,128)S(1)}, u32[]{:S(2)}, u32[]{:S(2)}) collective-permute-start(f32[4,3,2304]{2,0,1:T(4,128)} %param.3), channel_id=1, source_target_pairs={{144,0},{160,16},{176,32},{192,48},{208,64},{224,80},{240,96},{0,1... | collective-permute-start | bytes 331784 | tf_op jit(solution)/shard_map/ppermute | solution.py:14
  9.6 7.5 %collective-permute-start.7 = (f32[4,3,2304]{2,0,1:T(4,128)}, f32[4,3,2304]{2,0,1:T(4,128)S(1)}, u32[]{:S(2)}, u32[]{:S(2)}) collective-permute-start(f32[4,3,2304]{2,0,1:T(4,128)} %param.3), channel_id=1, source_target_pairs={{128,0},{144,16},{160,32},{176,48},{192,64},{208,80},{224,96},{240... | collective-permute-start | bytes 331784 | tf_op jit(solution)/shard_map/ppermute | solution.py:14
  19.7 2.3 copy-start
  22.0 131.5 %all-to-all-start = ((f32[16,9,3,2304]{3,2,1,0:T(4,128)}), f32[16,9,3,2304]{3,2,1,0:T(4,128)}, u32[]{:S(2)}, u32[]{:S(2)}) async-start(f32[16,9,3,2304]{3,2,1,0:T(4,128)} %bitcast.56), calls=%async_computation | async-start | bytes 10616832 | tf_op jit(solution)/shard_map/all_to_all | solution.py:62
  340.7 10.1 %copy-start.2 = (s32[4]{0:T(128)S(1)}, s32[4]{0:T(128)}, u32[]{:S(2)}) copy-start(s32[4]{0:T(128)} %param.4) | copy-start | bytes 52
  340.7 21.6 %copy-start.1 = (f32[4,3,2304]{2,0,1:T(4,128)S(1)}, f32[4,3,2304]{2,0,1:T(4,128)}, u32[]{:S(2)}) copy-start(f32[4,3,2304]{2,0,1:T(4,128)} %param.3) | copy-start | bytes 331780
  340.7 101.8 %all-to-all-start.1 = ((f32[1,9,48,2304]{3,0,1,2:T(1,128)}), f32[1,9,48,2304]{3,0,1,2:T(1,128)}, u32[]{:S(2)}, u32[]{:S(2)}) async-start(f32[1,9,48,2304]{3,0,1,2:T(1,128)} %copy.140), calls=%async_computation.1 | async-start | bytes 7962624 | tf_op jit(solution)/shard_map/all_to_all | solution.py:65
  350.8 11.7 %collective-permute-start.8 = (f32[4]{0:T(128)S(1)}, f32[4]{0:T(128)S(1)}, u32[]{:S(2)}, u32[]{:S(2)}) collective-permute-start(f32[4]{0:T(128)S(1)} %convert_multiply_fusion), channel_id=1, source_target_pairs={{240,0},{0,16},{16,32},{32,48},{48,64},{64,80},{80,96},{96,112},{1... | collective-permute-start | bytes 56 | tf_op jit(solution)/shard_map/ppermute | solution.py:14
  357.9 4.8 collective-permute-start.10
  357.9 7.9 %collective-permute-start.12 = (f32[4]{0:T(128)S(1)}, f32[4]{0:T(128)S(1)}, u32[]{:S(2)}, u32[]{:S(2)}) collective-permute-start(f32[4]{0:T(128)S(1)} %convert_multiply_fusion), channel_id=1, source_target_pairs={{208,0},{224,16},{240,32},{0,48},{16,64},{32,80},{48,96},{64,112},... | collective-permute-start | bytes 56 | tf_op jit(solution)/shard_map/ppermute | solution.py:14
  357.9 8.2 %collective-permute-start.14 = (f32[4]{0:T(128)S(1)}, f32[4]{0:T(128)S(1)}, u32[]{:S(2)}, u32[]{:S(2)}) collective-permute-start(f32[4]{0:T(128)S(1)} %convert_multiply_fusion), channel_id=1, source_target_pairs={{192,0},{208,16},{224,32},{240,48},{0,64},{16,80},{32,96},{48,112}... | collective-permute-start | bytes 56 | tf_op jit(solution)/shard_map/ppermute | solution.py:14
  362.3 4.9 %collective-permute-start.16 = (f32[4]{0:T(128)S(1)}, f32[4]{0:T(128)S(1)}, u32[]{:S(2)}, u32[]{:S(2)}) collective-permute-start(f32[4]{0:T(128)S(1)} %convert_multiply_fusion), channel_id=1, source_target_pairs={{176,0},{192,16},{208,32},{224,48},{240,64},{0,80},{16,96},{32,112... | collective-permute-start | bytes 56 | tf_op jit(solution)/shard_map/ppermute | solution.py:14
  362.5 4.9 %collective-permute-start.18 = (f32[4]{0:T(128)S(1)}, f32[4]{0:T(128)S(1)}, u32[]{:S(2)}, u32[]{:S(2)}) collective-permute-start(f32[4]{0:T(128)S(1)} %convert_multiply_fusion), channel_id=1, source_target_pairs={{160,0},{176,16},{192,32},{208,48},{224,64},{240,80},{0,96},{16,11... | collective-permute-start | bytes 56 | tf_op jit(solution)/shard_map/ppermute | solution.py:14
  362.7 5.1 %collective-permute-start.20 = (f32[4]{0:T(128)S(1)}, f32[4]{0:T(128)S(1)}, u32[]{:S(2)}, u32[]{:S(2)}) collective-permute-start(f32[4]{0:T(128)S(1)} %convert_multiply_fusion), channel_id=1, source_target_pairs={{144,0},{160,16},{176,32},{192,48},{208,64},{224,80},{240,96},{0,1... | collective-permute-start | bytes 56 | tf_op jit(solution)/shard_map/ppermute | solution.py:14
  365.8 92.4 %collective-permute-start.22 = (f32[4]{0:T(128)S(1)}, f32[4]{0:T(128)S(1)}, u32[]{:S(2)}, u32[]{:S(2)}) collective-permute-start(f32[4]{0:T(128)S(1)} %convert_multiply_fusion), channel_id=1, source_target_pairs={{128,0},{144,16},{160,32},{176,48},{192,64},{208,80},{224,96},{240... | collective-permute-start | bytes 56 | tf_op jit(solution)/shard_map/ppermute | solution.py:14
  453.2 11.3 %collective-permute-start.11 = (f32[4,3,2304]{2,1,0:T(4,128)S(1)}, f32[4,3,2304]{2,1,0:T(4,128)S(1)}, u32[]{:S(2)}, u32[]{:S(2)}) collective-permute-start(f32[4,3,2304]{2,1,0:T(4,128)S(1)} %get-tuple-element.40), channel_id=1, source_target_pairs={{32,0},{48,16},{64,32},{80,48},{96,64},{112,80},{128,96},{144,112}... | collective-permute-start | bytes 331784 | tf_op jit(solution)/shard_map/ppermute | solution.py:14
  453.3 18.4 %collective-permute-start.13 = (f32[4,3,2304]{2,1,0:T(4,128)S(1)}, f32[4,3,2304]{2,1,0:T(4,128)S(1)}, u32[]{:S(2)}, u32[]{:S(2)}) collective-permute-start(f32[4,3,2304]{2,1,0:T(4,128)S(1)} %get-tuple-element.29), channel_id=1, source_target_pairs={{48,0},{64,16},{80,32},{96,48},{112,64},{128,80},{144,96},{160,112... | collective-permute-start | bytes 331784 | tf_op jit(solution)/shard_map/ppermute | solution.py:14
  458.3 13.5 %collective-permute-start.15 = (f32[4,3,2304]{2,1,0:T(4,128)S(1)}, f32[4,3,2304]{2,1,0:T(4,128)S(1)}, u32[]{:S(2)}, u32[]{:S(2)}) collective-permute-start(f32[4,3,2304]{2,1,0:T(4,128)S(1)} %get-tuple-element.31), channel_id=1, source_target_pairs={{64,0},{80,16},{96,32},{112,48},{128,64},{144,80},{160,96},{176,11... | collective-permute-start | bytes 331784 | tf_op jit(solution)/shard_map/ppermute | solution.py:14
  462.3 9.5 %collective-permute-start.17 = (f32[4,3,2304]{2,1,0:T(4,128)S(1)}, f32[4,3,2304]{2,1,0:T(4,128)S(1)}, u32[]{:S(2)}, u32[]{:S(2)}) collective-permute-start(f32[4,3,2304]{2,1,0:T(4,128)S(1)} %get-tuple-element.33), channel_id=1, source_target_pairs={{80,0},{96,16},{112,32},{128,48},{144,64},{160,80},{176,96},{192,1... | collective-permute-start | bytes 331784 | tf_op jit(solution)/shard_map/ppermute | solution.py:14
  462.8 14.5 %collective-permute-start.19 = (f32[4,3,2304]{2,1,0:T(4,128)S(1)}, f32[4,3,2304]{2,1,0:T(4,128)S(1)}, u32[]{:S(2)}, u32[]{:S(2)}) collective-permute-start(f32[4,3,2304]{2,1,0:T(4,128)S(1)} %get-tuple-element.35), channel_id=1, source_target_pairs={{96,0},{112,16},{128,32},{144,48},{160,64},{176,80},{192,96},{208,... | collective-permute-start | bytes 331784 | tf_op jit(solution)/shard_map/ppermute | solution.py:14
  464.5 17.3 %collective-permute-start.21 = (f32[4,3,2304]{2,1,0:T(4,128)S(1)}, f32[4,3,2304]{2,1,0:T(4,128)S(1)}, u32[]{:S(2)}, u32[]{:S(2)}) collective-permute-start(f32[4,3,2304]{2,1,0:T(4,128)S(1)} %get-tuple-element.38), channel_id=1, source_target_pairs={{112,0},{128,16},{144,32},{160,48},{176,64},{192,80},{208,96},{224... | collective-permute-start | bytes 331784 | tf_op jit(solution)/shard_map/ppermute | solution.py:14
  471.6 10.2 %collective-permute-start.9 = (f32[4,3,2304]{2,1,0:T(4,128)S(1)}, f32[4,3,2304]{2,1,0:T(4,128)S(1)}, u32[]{:S(2)}, u32[]{:S(2)}) collective-permute-start(f32[4,3,2304]{2,1,0:T(4,128)S(1)} %get-tuple-element.6), channel_id=1, source_target_pairs={{16,0},{32,16},{48,32},{64,48},{80,64},{96,80},{112,96},{128,112},... | collective-permute-start | bytes 331784 | tf_op jit(solution)/shard_map/ppermute | solution.py:14
where the time goes:
time: 491 us; the launch traced here: 483 us
  waiting for transfers between devices  214 us (44%)
  local copies, waits for them, and re-layouts  131 us (27%)
  matrix products  72.2 us (15%)
  starting transfers between devices  59.4 us (12%)
  other arithmetic  5.73 us (1%)
    all_to_all x1, waiting for transfers between devices, solve_pairs(): lax.all_to_all(shaped, 'grid', split_axis=0, concat_axis=2, tiled=True)  118 us
    all_to_all x1, waiting for transfers between devices, solve_pairs(): lax.all_to_all(potential, 'grid', split_axis=2, concat_axis=0, tiled=True)  74.5 us
    dot_general x2, matrix products, apply_transform(): jnp.matmul(second.reshape(batch_size * extent * extent, extent), matrix.T...  40.5 us
    reshape x4, local copies, waits for them, and re-layouts, apply_transform(): first.reshape(batch_size * extent, extent, extent)  39.8 us
    ppermute x23, starting transfers between devices, shifted(): return lax.ppermute(block, axis, route)  39 us
    ppermute x23, waiting for transfers between devices, shifted(): return lax.ppermute(block, axis, route)  21.2 us
    reshape x2, local copies, waits for them, and re-layouts, apply_transform(): second.reshape(batch_size * extent * extent, extent)  18.4 us
    another operation x2, local copies, waits for them, and re-layouts, solve_pairs(): screened_potential(fields, transform, kernel).reshape(pieces.shape)  17.6 us
  transfers between devices with their start and end apart: 25, of which 10 were waited for; matrix products, arithmetic and copies ran while one was open for 3% of the time, Pallas kernels for 0%

commit v1 on v0

--- a/solution.py
+++ b/solution.py
@@ -59,7 +59,9 @@
     groups = lax.axis_size("grid")
     pair_count, planes, row_cells = densities.shape
     shaped = densities.reshape(groups, pair_count // groups, planes, row_cells)
-    pieces = lax.all_to_all(shaped, "grid", split_axis=0, concat_axis=2, tiled=True)
+    work_now = jnp.split(shaped, lax.axis_size("grid"), 0)
+    seen_now = lax.all_to_all(jnp.stack(work_now), "grid", 0, 0)
+    pieces = jnp.concatenate(seen_now, 2)
     fields = pieces.reshape(pieces.shape[1], pieces.shape[2], pieces.shape[3])
     potential = screened_potential(fields, transform, kernel).reshape(pieces.shape)
     sliced = lax.all_to_all(potential, "grid", split_axis=2, concat_axis=0, tiled=True)

time: 491 us -> 474 us (0.965)
  waiting for transfers between devices: 214 us -> 183 us
  local copies, waits for them, and re-layouts: 131 us -> 142 us
    all_to_all x1, waiting for transfers between devices: 118 us -> 89.1 us  [solve_pairs(): seen_now = lax.all_to_all(jnp.stack(work_now), 'grid', 0, 0)]
    unnamed x15 -> x20, local copies, waits for them, and re-layouts: 4.41 us -> 15.3 us
    another operation x0 -> x7, local copies, waits for them, and re-layouts: none -> 7.97 us  [the longest x1 6.81 us: solve_pairs(): fields = pieces.reshape(pieces.shape[1], pieces.shape[2], pieces.shape[3])]
    all_to_all x1 -> x0, local copies, waits for them, and re-layouts: 5.91 us -> none  [solve_pairs(): lax.all_to_all(shaped, 'grid', split_axis=0, concat_axis=2, tiled=True)]
where the time goes in v1:
time: 474 us; the launch traced here: 467 us
  waiting for transfers between devices  183 us (39%)
  local copies, waits for them, and re-layouts  142 us (30%)
  matrix products  72.4 us (15%)
  starting transfers between devices  61.1 us (13%)
  other arithmetic  6.51 us (1%)
    all_to_all x1, waiting for transfers between devices, solve_pairs(): seen_now = lax.all_to_all(jnp.stack(work_now), 'grid', 0, 0)  89.1 us
    all_to_all x1, waiting for transfers between devices, solve_pairs(): lax.all_to_all(potential, 'grid', split_axis=2, concat_axis=0, tiled=True)  73.6 us
    dot_general x2, matrix products, apply_transform(): jnp.matmul(second.reshape(batch_size * extent * extent, extent), matrix.T...  40.5 us
    ppermute x23, starting transfers between devices, shifted(): return lax.ppermute(block, axis, route)  40 us
    reshape x4, local copies, waits for them, and re-layouts, apply_transform(): first.reshape(batch_size * extent, extent, extent)  39.5 us
    ppermute x23, waiting for transfers between devices, shifted(): return lax.ppermute(block, axis, route)  20.7 us
    reshape x2, local copies, waits for them, and re-layouts, apply_transform(): second.reshape(batch_size * extent * extent, extent)  18.2 us
    another operation x2, local copies, waits for them, and re-layouts, solve_pairs(): screened_potential(fields, transform, kernel).reshape(pieces.shape)  17.6 us
  transfers between devices with their start and end apart: 25, of which 10 were waited for; matrix products, arithmetic and copies ran while one was open for 3% of the time, Pallas kernels for 0%

profile of v1, /device:TPU:7, one launch (start us, length us, event | category | flops | bytes accessed | tf_op | source)
XLA Modules:
  0.0 467.2 jit_solution(16686790904590908080)
XLA Ops:
  0.0 1.8 collective-permute-start
  1.8 1.2 collective-permute-start.1
  3.0 1.2 collective-permute-start.2
  4.2 2.4 collective-permute-start.3
  6.6 1.7 collective-permute-start.5
  8.3 1.2 collective-permute-start.6
  9.6 1.0 collective-permute-start.7
  10.5 1.0 copy.179
  11.7 2.0 collective-permute-done.4
  13.7 2.9 collective-permute-done.5
  17.2 1.2 broadcast_multiply_fusion
  19.5 0.9 copy_dynamic-update-slice_fusion.14
  20.4 1.0 copy_dynamic-update-slice_fusion.13
  21.4 1.0 copy_dynamic-update-slice_fusion.12
  22.4 0.9 copy_dynamic-update-slice_fusion.11
  23.3 1.0 copy_dynamic-update-slice_fusion.10
  24.3 1.0 copy_dynamic-update-slice_fusion.9
  25.2 0.9 copy_dynamic-update-slice_fusion.8
  26.2 0.9 copy_dynamic-update-slice_fusion.7
  27.1 1.0 copy_dynamic-update-slice_fusion.6
  28.1 0.9 copy_dynamic-update-slice_fusion.5
  29.0 1.0 copy_dynamic-update-slice_fusion.4
  30.0 1.0 copy_dynamic-update-slice_fusion.3
  30.9 1.0 copy_dynamic-update-slice_fusion.2
  31.9 1.0 copy_dynamic-update-slice_fusion.1
  32.9 1.0 copy_dynamic-update-slice_fusion
  33.8 0.9 reshape_dynamic-update-slice_fusion
  34.7 10.4 %all-to-all-start = ((f32[16,1,9,3,2304]{4,1,3,2,0:T(1,128)}), f32[16,1,9,3,2304]{4,1,3,2,0:T(1,128)}, u32[]{:S(2)}, u32[]{:S(2)}) async-start(f32[16,1,9,3,2304]{4,1,3,2,0:T(1,128)} %reshape_dynamic-update-slice_fusion), calls=%async_computation | async-start | bytes 7962624 | tf_op jit(solution)/shard_map/all_to_all | solution.py:63
  48.2 89.1 %all-to-all-done = f32[16,1,9,3,2304]{4,1,3,2,0:T(1,128)} async-done(((f32[16,1,9,3,2304]{4,1,3,2,0:T(1,128)}), f32[16,1,9,3,2304]{4,1,3,2,0:T(1,128)}, u32[]{:S(2)}, u32[]{:S(2)}) %all-to-all-start) | async-done | bytes 3981344 | tf_op jit(solution)/shard_map/all_to_all | solution.py:63
  137.2 5.8 %copy.204 = f32[1,9,16,3,2304]{4,3,2,1,0:T(4,128)} copy(f32[1,9,16,3,2304]{4,0,3,1,2:T(1,128)} %bitcast.27) | data formatting | bytes 7962624 | tf_op jit(solution)/shard_map/reshape | solution.py:64
  143.0 6.8 %reshape_reshape.9 = f32[9,48,2304]{2,1,0:T(8,128)} reshape(f32[1,9,16,3,2304]{4,3,2,1,0:T(4,128)} %copy.204) | data formatting | bytes 7962624 | tf_op jit(solution)/shard_map/reshape;reshape | solution.py:65
  149.9 7.7 %convolution_bitcast_fusion.1 = f32[9,48,2304]{2,1,0:T(8,128)} fusion(f32[9,48,2304]{2,1,0:T(8,128)} %reshape_reshape.9, s32[48]{0:T(128)S(1)} %add_select_fusion.1, pred[48]{0:T(512)(128)(4,1)S(1)} %iota_compare_fusion), kind=kOutput, calls=%fused_computation.1 | convolution fusion | flops 573331968 | bytes 7962864 | tf_op jit(solution)/shard_map/dot_general | solution.py:41
  157.6 10.3 %reshape.363 = f32[432,48,48]{2,1,0:T(8,128)} reshape(f32[9,48,2304]{2,1,0:T(8,128)} %convolution_bitcast_fusion.1) | data formatting | bytes 7962624 | tf_op jit(solution)/shard_map/reshape | solution.py:43
  167.8 9.5 %copy.207 = f32[432,48,48]{0,1,2:T(8,128)} copy(f32[432,48,48]{2,1,0:T(8,128)} %reshape.363) | data formatting | bytes 7962624 | tf_op jit(solution)/shard_map/reshape | solution.py:43
  177.3 7.9 %convolution_bitcast_fusion.3 = f32[432,48,48]{0,1,2:T(8,128)} fusion(f32[432,48,48]{0,1,2:T(8,128)} %copy.207, s32[48]{0:T(128)S(1)} %add_select_fusion.1, pred[48]{0:T(512)(128)(4,1)S(1)} %iota_compare_fusion), kind=kOutput, calls=%fused_computation.4 | convolution fusion | flops 573331968 | bytes 7962864 | tf_op jit(solution)/shard_map/dot_general | solution.py:42
  185.1 8.5 %copy.208 = f32[432,48,48]{1,0,2:T(8,128)} copy(f32[432,48,48]{0,1,2:T(8,128)} %convolution_bitcast_fusion.3) | data formatting | bytes 7962624 | tf_op jit(solution)/shard_map/transpose | solution.py:42
  193.6 9.1 %reshape.364 = f32[20736,48]{0,1:T(8,128)} reshape(f32[432,48,48]{1,0,2:T(8,128)} %copy.208) | data formatting | bytes 7962624 | tf_op jit(solution)/shard_map/reshape | solution.py:46
  202.7 20.2 %fusion.19 = f32[20736,48]{1,0:T(8,128)} fusion(f32[20736,48]{0,1:T(8,128)} %reshape.364, s32[48]{0:T(128)S(1)} %add_select_fusion.1, pred[48]{0:T(512)(128)(4,1)S(1)} %iota_compare_fusion), kind=kOutput, calls=%fused_computation.95 | convolution fusion | flops 573331968 | bytes 7962864 | tf_op jit(solution)/shard_map/dot_general | solution.py:45
  222.9 10.0 %reshape.365 = f32[9,48,2304]{2,1,0:T(8,128)} reshape(f32[20736,48]{1,0:T(8,128)} %fusion.19) | data formatting | bytes 7962624 | tf_op jit(solution)/shard_map/reshape | solution.py:50
  232.9 7.7 %convolution_bitcast_fusion = f32[9,48,2304]{2,1,0:T(8,128)} fusion(f32[9,48,2304]{2,1,0:T(8,128)} %reshape.365, f32[48,2304]{1,0:T(8,128)S(1)} %multiply_select_fusion, s32[48]{0:T(128)S(1)} %add_select_fusion.1, pred[48]{0:T(512)(128)(4,1)S(1)} %iota_compare_fusion), kind=kOutput, calls=%fused_computation | convolution fusion | flops 574327296 | bytes 8405232 | tf_op jit(solution)/shard_map/dot_general | solution.py:41
  240.5 10.3 %reshape.366 = f32[432,48,48]{2,1,0:T(8,128)} reshape(f32[9,48,2304]{2,1,0:T(8,128)} %convolution_bitcast_fusion) | data formatting | bytes 7962624 | tf_op jit(solution)/shard_map/reshape | solution.py:43
  250.8 9.5 %copy.210 = f32[432,48,48]{0,1,2:T(8,128)} copy(f32[432,48,48]{2,1,0:T(8,128)} %reshape.366) | data formatting | bytes 7962624 | tf_op jit(solution)/shard_map/reshape | solution.py:43
  260.3 8.6 %convolution_bitcast_fusion.2 = f32[432,48,48]{0,1,2:T(8,128)} fusion(f32[432,48,48]{0,1,2:T(8,128)} %copy.210, s32[48]{0:T(128)S(1)} %add_select_fusion.1, pred[48]{0:T(512)(128)(4,1)S(1)} %iota_compare_fusion), kind=kOutput, calls=%fused_computation.3 | convolution fusion | flops 573331968 | bytes 7962864 | tf_op jit(solution)/shard_map/dot_general | solution.py:42
  268.9 8.5 %copy.211 = f32[432,48,48]{1,0,2:T(8,128)} copy(f32[432,48,48]{0,1,2:T(8,128)} %convolution_bitcast_fusion.2) | data formatting | bytes 7962624 | tf_op jit(solution)/shard_map/transpose | solution.py:42
  277.4 9.1 %reshape.367 = f32[20736,48]{0,1:T(8,128)} reshape(f32[432,48,48]{1,0,2:T(8,128)} %copy.211) | data formatting | bytes 7962624 | tf_op jit(solution)/shard_map/reshape | solution.py:46
  286.5 20.3 %fusion.20 = f32[20736,48]{1,0:T(8,128)} fusion(f32[20736,48]{0,1:T(8,128)} %reshape.367, s32[48]{0:T(128)S(1)} %add_select_fusion.1, pred[48]{0:T(512)(128)(4,1)S(1)} %iota_compare_fusion), kind=kOutput, calls=%fused_computation.96 | convolution fusion | flops 573331968 | bytes 7962864 | tf_op jit(solution)/shard_map/dot_general | solution.py:45
  306.8 9.5 %reshape_reshape.10 = f32[1,9,48,2304]{3,2,1,0:T(8,128)} reshape(f32[20736,48]{1,0:T(8,128)} %fusion.20) | data formatting | bytes 7962624 | tf_op jit(solution)/shard_map/reshape;reshape | solution.py:66
  316.3 8.1 %copy.213 = f32[1,9,48,2304]{3,0,1,2:T(1,128)} copy(f32[1,9,48,2304]{3,2,1,0:T(8,128)} %reshape_reshape.10) | data formatting | bytes 7962624 | tf_op jit(solution)/shard_map/reshape;reshape | solution.py:66
  324.4 10.7 %all-to-all-start.1 = ((f32[1,9,48,2304]{3,0,1,2:T(1,128)}), f32[1,9,48,2304]{3,0,1,2:T(1,128)}, u32[]{:S(2)}, u32[]{:S(2)}) async-start(f32[1,9,48,2304]{3,0,1,2:T(1,128)} %copy.213), calls=%async_computation.1 | async-start | bytes 7962624 | tf_op jit(solution)/shard_map/all_to_all | solution.py:67
  335.1 6.4 %collective-permute-start.8 = (f32[4]{0:T(128)S(1)}, f32[4]{0:T(128)S(1)}, u32[]{:S(2)}, u32[]{:S(2)}) collective-permute-start(f32[4]{0:T(128)S(1)} %convert_multiply_fusion), channel_id=1, source_target_pairs={{240,0},{0,16},{16,32},{32,48},{48,64},{64,80},{80,96},{96,112},{1... | collective-permute-start | bytes 56 | tf_op jit(solution)/shard_map/ppermute | solution.py:14
  341.6 4.4 collective-permute-start.14
  346.4 2.9 collective-permute-start.20
  351.7 73.6 %all-to-all-done.1 = f32[1,9,48,2304]{3,0,1,2:T(1,128)} async-done(((f32[1,9,48,2304]{3,0,1,2:T(1,128)}), f32[1,9,48,2304]{3,0,1,2:T(1,128)}, u32[]{:S(2)}, u32[]{:S(2)}) %all-to-all-start.1) | async-done | bytes 3981344 | tf_op jit(solution)/shard_map/all_to_all | solution.py:67
  425.3 5.3 %copy.214 = f32[1,9,48,2304]{3,0,2,1:T(1,128)S(1)} copy(f32[1,9,48,2304]{3,0,1,2:T(1,128)} %all-to-all-done.1) | data formatting | bytes 7962624 | tf_op jit(solution)/shard_map/all_to_all | solution.py:67
  430.6 1.4 copy.215
  431.9 1.1 fusion.40
  433.1 2.9 multiply_reduce_fusion.14
  436.0 6.6 %collective-permute-start.13 = (f32[4,3,2304]{2,1,0:T(4,128)S(1)}, f32[4,3,2304]{2,1,0:T(4,128)S(1)}, u32[]{:S(2)}, u32[]{:S(2)}) collective-permute-start(f32[4,3,2304]{2,1,0:T(4,128)S(1)} %get-tuple-element.40), channel_id=1, source_target_pairs={{48,0},{64,16},{80,32},{96,48},{112,64},{128,80},{144,96},{160,112... | collective-permute-start | bytes 331784 | tf_op jit(solution)/shard_map/ppermute | solution.py:14
  442.8 3.4 collective-permute-start.15
  446.1 2.0 collective-permute-start.17
  448.2 3.2 collective-permute-start.21
  451.4 4.0 collective-permute-done.13
  455.5 6.0 %collective-permute-done.19 = f32[4,3,2304]{2,1,0:T(4,128)S(1)} collective-permute-done((f32[4,3,2304]{2,1,0:T(4,128)S(1)}, f32[4,3,2304]{2,1,0:T(4,128)S(1)}, u32[]{:S(2)}, u32[]{:S(2)}) %collective-permute-start.19) | collective-permute-done | bytes 110624 | tf_op jit(solution)/shard_map/ppermute | solution.py:14
  461.5 4.3 collective-permute-done.21
  (82 shorter events, 8.2 us)
Async XLA Ops:
  0.0 6.6 %collective-permute-start = (f32[4,3,2304]{2,0,1:T(4,128)}, f32[4,3,2304]{2,0,1:T(4,128)S(1)}, u32[]{:S(2)}, u32[]{:S(2)}) collective-permute-start(f32[4,3,2304]{2,0,1:T(4,128)} %param.3), channel_id=1, source_target_pairs={{240,0},{0,16},{16,32},{32,48},{48,64},{64,80},{80,96},{96,112},{1... | collective-permute-start | bytes 331784 | tf_op jit(solution)/shard_map/ppermute | solution.py:14
  1.8 6.5 %collective-permute-start.1 = (f32[4,3,2304]{2,0,1:T(4,128)}, f32[4,3,2304]{2,0,1:T(4,128)S(1)}, u32[]{:S(2)}, u32[]{:S(2)}) collective-permute-start(f32[4,3,2304]{2,0,1:T(4,128)} %param.3), channel_id=1, source_target_pairs={{224,0},{240,16},{0,32},{16,48},{32,64},{48,80},{64,96},{80,112},{... | collective-permute-start | bytes 331784 | tf_op jit(solution)/shard_map/ppermute | solution.py:14
  3.0 6.6 %collective-permute-start.2 = (f32[4,3,2304]{2,0,1:T(4,128)}, f32[4,3,2304]{2,0,1:T(4,128)S(1)}, u32[]{:S(2)}, u32[]{:S(2)}) collective-permute-start(f32[4,3,2304]{2,0,1:T(4,128)} %param.3), channel_id=1, source_target_pairs={{208,0},{224,16},{240,32},{0,48},{16,64},{32,80},{48,96},{64,112},... | collective-permute-start | bytes 331784 | tf_op jit(solution)/shard_map/ppermute | solution.py:14
  4.2 7.5 %collective-permute-start.3 = (f32[4,3,2304]{2,0,1:T(4,128)}, f32[4,3,2304]{2,0,1:T(4,128)S(1)}, u32[]{:S(2)}, u32[]{:S(2)}) collective-permute-start(f32[4,3,2304]{2,0,1:T(4,128)} %param.3), channel_id=1, source_target_pairs={{192,0},{208,16},{224,32},{240,48},{0,64},{16,80},{32,96},{48,112}... | collective-permute-start | bytes 331784 | tf_op jit(solution)/shard_map/ppermute | solution.py:14
  6.6 7.1 %collective-permute-start.4 = (f32[4,3,2304]{2,0,1:T(4,128)}, f32[4,3,2304]{2,0,1:T(4,128)S(1)}, u32[]{:S(2)}, u32[]{:S(2)}) collective-permute-start(f32[4,3,2304]{2,0,1:T(4,128)} %param.3), channel_id=1, source_target_pairs={{176,0},{192,16},{208,32},{224,48},{240,64},{0,80},{16,96},{32,112... | collective-permute-start | bytes 331784 | tf_op jit(solution)/shard_map/ppermute | solution.py:14
  6.6 10.0 %collective-permute-start.5 = (f32[4,3,2304]{2,0,1:T(4,128)}, f32[4,3,2304]{2,0,1:T(4,128)S(1)}, u32[]{:S(2)}, u32[]{:S(2)}) collective-permute-start(f32[4,3,2304]{2,0,1:T(4,128)} %param.3), channel_id=1, source_target_pairs={{160,0},{176,16},{192,32},{208,48},{224,64},{240,80},{0,96},{16,11... | collective-permute-start | bytes 331784 | tf_op jit(solution)/shard_map/ppermute | solution.py:14
  8.3 8.8 %collective-permute-start.6 = (f32[4,3,2304]{2,0,1:T(4,128)}, f32[4,3,2304]{2,0,1:T(4,128)S(1)}, u32[]{:S(2)}, u32[]{:S(2)}) collective-permute-start(f32[4,3,2304]{2,0,1:T(4,128)} %param.3), channel_id=1, source_target_pairs={{144,0},{160,16},{176,32},{192,48},{208,64},{224,80},{240,96},{0,1... | collective-permute-start | bytes 331784 | tf_op jit(solution)/shard_map/ppermute | solution.py:14
  9.6 7.5 %collective-permute-start.7 = (f32[4,3,2304]{2,0,1:T(4,128)}, f32[4,3,2304]{2,0,1:T(4,128)S(1)}, u32[]{:S(2)}, u32[]{:S(2)}) collective-permute-start(f32[4,3,2304]{2,0,1:T(4,128)} %param.3), channel_id=1, source_target_pairs={{128,0},{144,16},{160,32},{176,48},{192,64},{208,80},{224,96},{240... | collective-permute-start | bytes 331784 | tf_op jit(solution)/shard_map/ppermute | solution.py:14
  34.7 102.6 %all-to-all-start = ((f32[16,1,9,3,2304]{4,1,3,2,0:T(1,128)}), f32[16,1,9,3,2304]{4,1,3,2,0:T(1,128)}, u32[]{:S(2)}, u32[]{:S(2)}) async-start(f32[16,1,9,3,2304]{4,1,3,2,0:T(1,128)} %reshape_dynamic-update-slice_fusion), calls=%async_computation | async-start | bytes 7962624 | tf_op jit(solution)/shard_map/all_to_all | solution.py:63
  324.4 10.7 %copy-start.1 = (s32[4]{0:T(128)S(1)}, s32[4]{0:T(128)}, u32[]{:S(2)}) copy-start(s32[4]{0:T(128)} %param.4) | copy-start | bytes 52
  324.4 21.6 %copy-start = (f32[4,3,2304]{2,0,1:T(4,128)S(1)}, f32[4,3,2304]{2,0,1:T(4,128)}, u32[]{:S(2)}) copy-start(f32[4,3,2304]{2,0,1:T(4,128)} %param.3) | copy-start | bytes 331780
  324.4 100.8 %all-to-all-start.1 = ((f32[1,9,48,2304]{3,0,1,2:T(1,128)}), f32[1,9,48,2304]{3,0,1,2:T(1,128)}, u32[]{:S(2)}, u32[]{:S(2)}) async-start(f32[1,9,48,2304]{3,0,1,2:T(1,128)} %copy.213), calls=%async_computation.1 | async-start | bytes 7962624 | tf_op jit(solution)/shard_map/all_to_all | solution.py:67
  335.1 11.0 %collective-permute-start.8 = (f32[4]{0:T(128)S(1)}, f32[4]{0:T(128)S(1)}, u32[]{:S(2)}, u32[]{:S(2)}) collective-permute-start(f32[4]{0:T(128)S(1)} %convert_multiply_fusion), channel_id=1, source_target_pairs={{240,0},{0,16},{16,32},{32,48},{48,64},{64,80},{80,96},{96,112},{1... | collective-permute-start | bytes 56 | tf_op jit(solution)/shard_map/ppermute | solution.py:14
  341.6 4.8 %collective-permute-start.10 = (f32[4]{0:T(128)S(1)}, f32[4]{0:T(128)S(1)}, u32[]{:S(2)}, u32[]{:S(2)}) collective-permute-start(f32[4]{0:T(128)S(1)} %convert_multiply_fusion), channel_id=1, source_target_pairs={{224,0},{240,16},{0,32},{16,48},{32,64},{48,80},{64,96},{80,112},{... | collective-permute-start | bytes 56 | tf_op jit(solution)/shard_map/ppermute | solution.py:14
  341.6 7.9 %collective-permute-start.12 = (f32[4]{0:T(128)S(1)}, f32[4]{0:T(128)S(1)}, u32[]{:S(2)}, u32[]{:S(2)}) collective-permute-start(f32[4]{0:T(128)S(1)} %convert_multiply_fusion), channel_id=1, source_target_pairs={{208,0},{224,16},{240,32},{0,48},{16,64},{32,80},{48,96},{64,112},... | collective-permute-start | bytes 56 | tf_op jit(solution)/shard_map/ppermute | solution.py:14
  341.6 8.4 %collective-permute-start.14 = (f32[4]{0:T(128)S(1)}, f32[4]{0:T(128)S(1)}, u32[]{:S(2)}, u32[]{:S(2)}) collective-permute-start(f32[4]{0:T(128)S(1)} %convert_multiply_fusion), channel_id=1, source_target_pairs={{192,0},{208,16},{224,32},{240,48},{0,64},{16,80},{32,96},{48,112}... | collective-permute-start | bytes 56 | tf_op jit(solution)/shard_map/ppermute | solution.py:14
  346.0 4.9 %collective-permute-start.16 = (f32[4]{0:T(128)S(1)}, f32[4]{0:T(128)S(1)}, u32[]{:S(2)}, u32[]{:S(2)}) collective-permute-start(f32[4]{0:T(128)S(1)} %convert_multiply_fusion), channel_id=1, source_target_pairs={{176,0},{192,16},{208,32},{224,48},{240,64},{0,80},{16,96},{32,112... | collective-permute-start | bytes 56 | tf_op jit(solution)/shard_map/ppermute | solution.py:14
  346.2 4.9 %collective-permute-start.18 = (f32[4]{0:T(128)S(1)}, f32[4]{0:T(128)S(1)}, u32[]{:S(2)}, u32[]{:S(2)}) collective-permute-start(f32[4]{0:T(128)S(1)} %convert_multiply_fusion), channel_id=1, source_target_pairs={{160,0},{176,16},{192,32},{208,48},{224,64},{240,80},{0,96},{16,11... | collective-permute-start | bytes 56 | tf_op jit(solution)/shard_map/ppermute | solution.py:14
  346.4 5.1 %collective-permute-start.20 = (f32[4]{0:T(128)S(1)}, f32[4]{0:T(128)S(1)}, u32[]{:S(2)}, u32[]{:S(2)}) collective-permute-start(f32[4]{0:T(128)S(1)} %convert_multiply_fusion), channel_id=1, source_target_pairs={{144,0},{160,16},{176,32},{192,48},{208,64},{224,80},{240,96},{0,1... | collective-permute-start | bytes 56 | tf_op jit(solution)/shard_map/ppermute | solution.py:14
  349.5 93.2 %collective-permute-start.22 = (f32[4]{0:T(128)S(1)}, f32[4]{0:T(128)S(1)}, u32[]{:S(2)}, u32[]{:S(2)}) collective-permute-start(f32[4]{0:T(128)S(1)} %convert_multiply_fusion), channel_id=1, source_target_pairs={{128,0},{144,16},{160,32},{176,48},{192,64},{208,80},{224,96},{240... | collective-permute-start | bytes 56 | tf_op jit(solution)/shard_map/ppermute | solution.py:14
  435.9 12.3 %collective-permute-start.11 = (f32[4,3,2304]{2,1,0:T(4,128)S(1)}, f32[4,3,2304]{2,1,0:T(4,128)S(1)}, u32[]{:S(2)}, u32[]{:S(2)}) collective-permute-start(f32[4,3,2304]{2,1,0:T(4,128)S(1)} %get-tuple-element.51), channel_id=1, source_target_pairs={{32,0},{48,16},{64,32},{80,48},{96,64},{112,80},{128,96},{144,112}... | collective-permute-start | bytes 331784 | tf_op jit(solution)/shard_map/ppermute | solution.py:14
  436.0 19.3 %collective-permute-start.13 = (f32[4,3,2304]{2,1,0:T(4,128)S(1)}, f32[4,3,2304]{2,1,0:T(4,128)S(1)}, u32[]{:S(2)}, u32[]{:S(2)}) collective-permute-start(f32[4,3,2304]{2,1,0:T(4,128)S(1)} %get-tuple-element.40), channel_id=1, source_target_pairs={{48,0},{64,16},{80,32},{96,48},{112,64},{128,80},{144,96},{160,112... | collective-permute-start | bytes 331784 | tf_op jit(solution)/shard_map/ppermute | solution.py:14
  442.8 12.7 %collective-permute-start.15 = (f32[4,3,2304]{2,1,0:T(4,128)S(1)}, f32[4,3,2304]{2,1,0:T(4,128)S(1)}, u32[]{:S(2)}, u32[]{:S(2)}) collective-permute-start(f32[4,3,2304]{2,1,0:T(4,128)S(1)} %get-tuple-element.42), channel_id=1, source_target_pairs={{64,0},{80,16},{96,32},{112,48},{128,64},{144,80},{160,96},{176,11... | collective-permute-start | bytes 331784 | tf_op jit(solution)/shard_map/ppermute | solution.py:14
  446.1 9.4 %collective-permute-start.17 = (f32[4,3,2304]{2,1,0:T(4,128)S(1)}, f32[4,3,2304]{2,1,0:T(4,128)S(1)}, u32[]{:S(2)}, u32[]{:S(2)}) collective-permute-start(f32[4,3,2304]{2,1,0:T(4,128)S(1)} %get-tuple-element.44), channel_id=1, source_target_pairs={{80,0},{96,16},{112,32},{128,48},{144,64},{160,80},{176,96},{192,1... | collective-permute-start | bytes 331784 | tf_op jit(solution)/shard_map/ppermute | solution.py:14
  448.1 13.4 %collective-permute-start.19 = (f32[4,3,2304]{2,1,0:T(4,128)S(1)}, f32[4,3,2304]{2,1,0:T(4,128)S(1)}, u32[]{:S(2)}, u32[]{:S(2)}) collective-permute-start(f32[4,3,2304]{2,1,0:T(4,128)S(1)} %get-tuple-element.46), channel_id=1, source_target_pairs={{96,0},{112,16},{128,32},{144,48},{160,64},{176,80},{192,96},{208,... | collective-permute-start | bytes 331784 | tf_op jit(solution)/shard_map/ppermute | solution.py:14
  448.2 17.6 %collective-permute-start.21 = (f32[4,3,2304]{2,1,0:T(4,128)S(1)}, f32[4,3,2304]{2,1,0:T(4,128)S(1)}, u32[]{:S(2)}, u32[]{:S(2)}) collective-permute-start(f32[4,3,2304]{2,1,0:T(4,128)S(1)} %get-tuple-element.49), channel_id=1, source_target_pairs={{112,0},{128,16},{144,32},{160,48},{176,64},{192,80},{208,96},{224... | collective-permute-start | bytes 331784 | tf_op jit(solution)/shard_map/ppermute | solution.py:14
  455.3 10.5 %collective-permute-start.9 = (f32[4,3,2304]{2,1,0:T(4,128)S(1)}, f32[4,3,2304]{2,1,0:T(4,128)S(1)}, u32[]{:S(2)}, u32[]{:S(2)}) collective-permute-start(f32[4,3,2304]{2,1,0:T(4,128)S(1)} %get-tuple-element.6), channel_id=1, source_target_pairs={{16,0},{32,16},{48,32},{64,48},{80,64},{96,80},{112,96},{128,112},... | collective-permute-start | bytes 331784 | tf_op jit(solution)/shard_map/ppermute | solution.py:14
